TPU v7x, 32 devices: a whole 2x2x4 slice. The times are simulated.
32 devices in a mesh: src: 16 (over z, y, x), hid: 2 (over core).
Axes of the slice: x: 2, y: 2, z: 4, core: 2. Of those that a mesh axis runs over, the one named last changes fastest.
Arguments:
- source_field: float32 [128, 2, 98, 128], P('src'), may hold values from -36 to 36
- hidden_gain: float32 [98], replicated, may hold values from 0.1 to 1.9
- enc_tiles: float32 [1024, 128, 128], P(('src', 'hid')), may hold values from -0.25 to 0.25
- enc_src_block: int32 [1024], P(('src', 'hid')), may hold values from 0 to 127, as said below
- enc_hid_block: int32 [1024], P(('src', 'hid')), may hold values from 0 to 63, as said below
- enc_count: int32 [32], P(('src', 'hid')), may hold values from 1 to 32, as said below
- dec_tiles: float32 [1024, 128, 128], P(('src', 'hid')), may hold values from -0.15625 to 0.15625
- dec_src_block: int32 [1024], P(('src', 'hid')), may hold values from 0 to 127, as said below
- dec_hid_block: int32 [1024], P(('src', 'hid')), may hold values from 0 to 63, as said below
- dec_count: int32 [32], P(('src', 'hid')), may hold values from 1 to 32, as said below
Outputs:
- returned: float32 [128, 2, 98, 128], P('src')
- channel_rms: float32 [98], replicated
Inputs may be any that keep to these rules, and one draw needn't show every extreme that they name: `enc_src_block`: the 32 entries starting at (s * 2 + h) * 32 lie in s * 8 to (s + 1) * 8 - 1. `enc_hid_block`: the 32 entries starting at (s * 2 + h) * 32 lie in h * 32 to (h + 1) * 32 - 1; within these entries no pair (enc_src_block, enc_hid_block) repeats. `enc_count`: entry s * 2 + h counts the live slots of that group; it equals 32 for some group. `dec_src_block`: the 32 entries starting at (s * 2 + h) * 32 lie in s * 8 to (s + 1) * 8 - 1. `dec_hid_block`: the 32 entries starting at (s * 2 + h) * 32 lie in h * 32 to (h + 1) * 32 - 1; within these entries no pair (dec_src_block, dec_hid_block) repeats. `dec_count`: entry s * 2 + h counts the live slots of that group; it equals 32 for some group.
All inputs are finite; a program needn't handle non-finite values.
Results may differ from a plain program's by a relative error of at most 0.0003.
Values sent between devices are 32-bit elements; how exact they have to be, the bound alone decides.
No kernel may reach another device: no remote copies, remote signals or barrier semaphores. Data moves between devices by JAX's collectives and lax.ppermute only.
A program may use at most 64 MiB of HBM per device.

v0:
```python
import jax
import jax.numpy as jnp
from jax import lax
from jax.sharding import PartitionSpec as P

HID_BLK = 32
GROUP = 16
HIGH = lax.Precision.HIGHEST
EPSILON = 1e-06


def normalize(total, gain, batch, channels):
    nodes, features, width = total.shape
    grouped = total.reshape(nodes, batch, channels, width)
    mean_square = jnp.mean(grouped * grouped, axis=2, keepdims=True)
    scaled = grouped * gain[None, None, :, None] * lax.rsqrt(mean_square + EPSILON)
    return scaled.reshape(nodes, features, width)


def body(
    source_field,
    hidden_gain,
    enc_tiles,
    enc_src_block,
    enc_hid_block,
    enc_count,
    dec_tiles,
    dec_src_block,
    dec_hid_block,
    dec_count,
):
    src_blocks, batch, channels, width = source_field.shape
    features = batch * channels
    flat = source_field.reshape(src_blocks, features, width)
    src_first = lax.axis_index("src") * src_blocks
    hid_first = lax.axis_index("hid") * HID_BLK
    enc_sources = enc_src_block - src_first
    enc_targets = enc_hid_block - hid_first
    dec_targets = dec_src_block - src_first
    dec_sources = dec_hid_block - hid_first
    src_range = jnp.arange(src_blocks, dtype=jnp.int32)
    hid_range = jnp.arange(HID_BLK, dtype=jnp.int32)
    slot_range = jnp.arange(GROUP, dtype=jnp.int32)

    def encode_group(step, partial_value):
        start = step * GROUP
        tiles = lax.dynamic_slice_in_dim(enc_tiles, start, GROUP, 0)
        sources = lax.dynamic_slice_in_dim(enc_sources, start, GROUP, 0)
        targets = lax.dynamic_slice_in_dim(enc_targets, start, GROUP, 0)
        alive = (start + slot_range < enc_count[0])[:, None]
        select = (sources[:, None] == src_range[None, :]).astype(jnp.float32)
        placing = (alive & (targets[:, None] == hid_range[None, :])).astype(jnp.float32)
        blocks = jnp.einsum("ts,sfc->tfc", select, flat, precision=HIGH)
        product = jnp.einsum("tfr,trc->tfc", blocks, tiles, precision=HIGH)
        return partial_value + jnp.einsum("th,tfc->hfc", placing, product, precision=HIGH)

    enc_groups = (enc_count[0] + GROUP - 1) // GROUP
    partial_value = lax.fori_loop(
        0, enc_groups, encode_group, jnp.zeros((HID_BLK, features, width), jnp.float32)
    )
    hidden = normalize(lax.psum(partial_value, "src"), hidden_gain, batch, channels)

    def fetch(start):
        sources = lax.dynamic_slice_in_dim(dec_sources, start, GROUP, 0)
        select = (sources[:, None] == hid_range[None, :]).astype(jnp.float32)
        return jnp.einsum("th,hfc->tfc", select, hidden, precision=HIGH)

    def decode_group(step, partial_back):
        start = step * GROUP
        tiles = lax.dynamic_slice_in_dim(dec_tiles, start, GROUP, 0)
        targets = lax.dynamic_slice_in_dim(dec_targets, start, GROUP, 0)
        alive = (start + slot_range < dec_count[0])[:, None]
        blocks = fetch(start)
        product = jnp.einsum("tfr,trc->tfc", blocks, tiles, precision=HIGH)
        placing = (alive & (targets[:, None] == src_range[None, :])).astype(jnp.float32)
        return partial_back + jnp.einsum("ts,tfc->sfc", placing, product, precision=HIGH)

    dec_groups = (dec_count[0] + GROUP - 1) // GROUP
    partial_back = lax.fori_loop(
        0, dec_groups, decode_group, jnp.zeros((src_blocks, features, width), jnp.float32)
    )
    total_points = src_blocks * lax.axis_size("src") * batch * width
    returned = lax.psum(partial_back, "hid")
    difference = returned - flat
    squares = jnp.sum(
        (difference * difference).reshape(src_blocks, batch, channels, width), axis=(0, 1, 3)
    )
    sums = lax.psum(squares, "src")
    channel_rms = jnp.sqrt(sums / total_points + EPSILON)
    return (returned.reshape(source_field.shape), channel_rms)


def solution(mesh):
    in_specs = (
        P("src", None, None, None),
        P(),
        P(("src", "hid"), None, None),
        P(("src", "hid")),
        P(("src", "hid")),
        P(("src", "hid")),
        P(("src", "hid"), None, None),
        P(("src", "hid")),
        P(("src", "hid")),
        P(("src", "hid")),
    )
    out_specs = (P("src", None, None, None), P())
    return jax.shard_map(body, mesh=mesh, in_specs=in_specs, out_specs=out_specs, check_vma=False)
```

profile of v0, /device:TPU:0, one launch (start us, length us, event | category | flops | bytes accessed | tf_op | source)
XLA Modules:
  0.0 277.2 jit_solution(4805491269484964007)
XLA Ops:
  7.2 0.0 all-reduce.3.cloned.1.call-start
  7.9 2.1 copy.23
  10.0 0.7 broadcast_subtract_fusion
  10.6 0.4 broadcast_in_dim.5
  11.0 8.7 %while.22 = (s32[]{:T(128)}, f32[32,196,128]{2,0,1:T(8,128)S(1)}, s32[]{:T(128)}, s32[1]{0:T(128)}, s32[32]{0:T(128)S(1)}, /*index=5*/s32[32]{0:T(128)S(1)}, f32...) while((s32[]{:T(128)}, f32[32,196,128]{2,0,1:T(8,128)S(1)}, ...), condition=%wide.region_1.2_spmd.clone, body=%wide.region_0.1_spmd.clone.sunk | while | flops 810042496 | bytes 23085684 | solution.py:58
  11.1 0.0 copy-start.1
  11.1 0.1 dynamic_slice.35
  11.2 2.1 fusion.73
  13.3 0.0 copy-done.1
  13.3 3.2 %fusion.74 = f32[16,196,128]{2,1,0:T(8,128)S(1)} fusion(f32[16,196,128]{2,0,1:T(8,128)S(1)} %fusion.73, f32[32,128,128]{2,1,0:T(8,128)S(1)} %copy-done.1, s32[]{:T(128)S(6)} %select_n.24), kind=kOutput, calls=%fused_computation.7.clone.1 | convolution fusion | flops 616562688 | bytes 4259844 | tf_op jit(solution)/shard_map/while/body/tfr,trc->tfc/dot_general | solution.py:54
  16.5 0.1 dynamic_slice.36
  16.5 0.7 fusion.75
  17.2 2.6 convolution_add_fusion.2
  19.8 0.0 copy-start
  19.8 0.0 copy-start.6
  19.8 0.0 copy-start.4
  19.8 0.0 copy-start.5
  19.8 1.7 copy-done
  21.5 0.0 all-reduce.3.cloned.1.call-update
  21.5 0.0 all-reduce.5.cloned.1.call-start
  22.2 0.0 copy-done.6
  22.2 0.1 mul.48
  22.3 0.0 copy-done.4
  22.3 0.0 copy-done.5
  22.3 159.6 %all-reduce.3.cloned.1.call-done = f32[32,196,128]{2,0,1:T(8,128)} async-done(((f32[32,196,128]{2,0,1:T(8,128)}), f32[32,196,128]{2,0,1:T(8,128)}) %all-reduce.3.cloned.1.call-update) | async-done | bytes 3211280 | tf_op jit(solution)/shard_map/psum | solution.py:61
  181.9 3.6 %mul.51 = f32[32,196,128]{2,0,1:T(8,128)S(1)} multiply(f32[32,196,128]{2,0,1:T(8,128)} %all-reduce.3.cloned.1.call-done, f32[32,196,128]{2,0,1:T(8,128)} %all-reduce.3.cloned.1.call-done) | non-fusion elementwise | flops 802816 | bytes 9633792 | tf_op jit(solution)/shard_map/mul | solution.py:15
  185.5 0.2 reduce_sum.21
  185.8 2.2 bitcast_multiply_fusion
  188.0 0.9 broadcast_in_dim.4
  188.9 16.7 %while.23 = (s32[]{:T(128)}, f32[8,196,128]{2,0,1:T(8,128)}, s32[]{:T(128)}, s32[1]{0:T(128)}, s32[32]{0:T(128)S(1)}, /*index=5*/s32[32]{0:T(128)S(1)}, f32[32,1...) while((s32[]{:T(128)}, f32[8,196,128]{2,0,1:T(8,128)}, ...), condition=%wide.region_5.6_spmd.clone, body=%wide.region_4.5_spmd.clone.sunk | while | flops 809440000 | bytes 20677236 | solution.py:79
  188.9 0.1 dynamic_slice.38
  189.0 0.0 copy-start.2
  189.0 1.2 fusion.82
  190.3 0.3 copy-done.2
  190.6 3.2 %fusion.83 = f32[16,196,128]{2,1,0:T(8,128)S(1)} fusion(f32[16,196,128]{2,0,1:T(8,128)S(1)} %fusion.82, f32[32,128,128]{2,1,0:T(8,128)S(1)} %copy-done.2, s32[]{:T(128)S(6)} %select_n.25), kind=kOutput, calls=%fused_computation.23.clone.1 | convolution fusion | flops 616562688 | bytes 4259844 | tf_op jit(solution)/shard_map/while/body/tfr,trc->tfc/dot_general | solution.py:74
  193.8 0.1 dynamic_slice.39
  193.8 0.7 fusion.84
  194.5 2.8 %fusion.85 = f32[8,196,128]{2,0,1:T(8,128)} fusion(f32[8,196,128]{2,0,1:T(8,128)} %get-tuple-element.375, f32[16,196,128]{2,1,0:T(8,128)S(1)} %fusion.83, s32[16]{0:T(128)S(1)} %dynamic_slice.39, pred[16]{0:T(512)(128)(4,1)S(1)} %fusion.84), kind=kOutput, calls=%fused_computation.27.clone.1 | convolution fusion | flops 38736128 | bytes 3211344 | tf_op jit(solution)/shard_map/while/body/ts,tfc->sfc/dot_general | solution.py:76
  197.3 0.1 dynamic_slice.38
  197.4 0.0 copy-start.2
  197.4 1.2 fusion.82
  198.6 0.3 copy-done.2
  199.0 3.2 %fusion.83 = f32[16,196,128]{2,1,0:T(8,128)S(1)} fusion(f32[16,196,128]{2,0,1:T(8,128)S(1)} %fusion.82, f32[32,128,128]{2,1,0:T(8,128)S(1)} %copy-done.2, s32[]{:T(128)S(6)} %select_n.25), kind=kOutput, calls=%fused_computation.23.clone.1 | convolution fusion | flops 616562688 | bytes 4259844 | tf_op jit(solution)/shard_map/while/body/tfr,trc->tfc/dot_general | solution.py:74
  202.1 0.1 dynamic_slice.39
  202.2 0.7 fusion.84
  202.9 2.8 %fusion.85 = f32[8,196,128]{2,0,1:T(8,128)} fusion(f32[8,196,128]{2,0,1:T(8,128)} %get-tuple-element.375, f32[16,196,128]{2,1,0:T(8,128)S(1)} %fusion.83, s32[16]{0:T(128)S(1)} %dynamic_slice.39, pred[16]{0:T(512)(128)(4,1)S(1)} %fusion.84), kind=kOutput, calls=%fused_computation.27.clone.1 | convolution fusion | flops 38736128 | bytes 3211344 | tf_op jit(solution)/shard_map/while/body/ts,tfc->sfc/dot_general | solution.py:76
  205.6 0.0 all-reduce.5.cloned.1.call-update
  205.7 18.3 %all-reduce.5.cloned.1.call-done = f32[8,196,128]{2,0,1:T(8,128)} async-done(((f32[8,196,128]{2,0,1:T(8,128)}), f32[8,196,128]{2,0,1:T(8,128)}) %all-reduce.5.cloned.1.call-update) | async-done | bytes 802832 | tf_op jit(solution)/shard_map/psum | solution.py:83
  224.0 0.0 copy-start.3
  224.0 2.5 multiply_reduce_fusion
  226.4 0.1 reduce_sum.27
  226.5 42.0 %psum.23 = f32[98]{0:T(128)S(1)} all-reduce(f32[98]{0:T(128)S(1)} %reduce_sum.28), channel_id=1, replica_groups=mesh['src'=16,'hid'=2] {'src'}, use_global_device_ids=true, to_apply=%region_9.10 | all-reduce | flops 98 | bytes 784 | tf_op jit(solution)/shard_map/psum | solution.py:88
  268.5 0.5 add_sqrt_fusion
  269.1 0.0 copy-done.3
  269.1 1.3 copy.24
  (4 shorter events, 0.0 us)
Async XLA Ops:
  7.2 174.7 %all-reduce.3.cloned.1.call-start = ((), (), s32[]{:S(2)}) async-start(), calls=%async_computation | async-start | bytes 6422528 | tf_op jit(solution)/shard_map/psum | solution.py:61
  11.1 2.2 copy-start.1
  19.8 1.7 copy-start
  19.8 2.4 copy-start.6
  19.8 2.5 copy-start.4
  19.8 2.5 copy-start.5
  21.5 202.4 %all-reduce.5.cloned.1.call-start = ((), (), s32[]{:S(2)}) async-start(), calls=%async_computation.1 | async-start | bytes 1605632 | tf_op jit(solution)/shard_map/psum | solution.py:83
  189.0 1.6 copy-start.2
  197.4 1.6 copy-start.2
  224.0 45.1 %copy-start.3 = (f32[8,196,128]{2,0,1:T(8,128)S(1)}, f32[8,196,128]{2,0,1:T(8,128)}, u32[]{:S(2)}) copy-start(f32[8,196,128]{2,0,1:T(8,128)} %all-reduce.5.cloned.1.call-done) | copy-start | bytes 2408452
Sparse Core Ops, SparseCore 0:
  21.6 160.2 all-reduce.2
  205.8 18.1 all-reduce.4
where the time goes:
time: 278 us; the launch traced here: 277 us
  waiting for transfers between devices  178 us (64%)
  blocking collectives  42 us (15%)
  matrix products  22.2 us (8%)
  between operations  15.5 us (6%)
  other arithmetic  11.8 us (4%)
  local copies, waits for them, and re-layouts  7.73 us (3%)
    psum x1, waiting for transfers between devices, body(): lax.psum(partial_value, 'src')  160 us
    psum x1, blocking collectives, body(): sums = lax.psum(squares, 'src')  42 us
    psum x1, waiting for transfers between devices, body(): returned = lax.psum(partial_back, 'hid')  18.3 us
    dot_general x2, matrix products, decode_group(): product = jnp.einsum('tfr,trc->tfc', blocks, tiles, precision=HIGH)  6.31 us
    dot_general x2, matrix products, decode_group(): jnp.einsum('ts,tfc->sfc', placing, product, precision=HIGH)  5.57 us
  transfers between devices with their start and end apart: 2, of which 2 were waited for; matrix products, arithmetic and copies ran while one was open for 0% of the time, Pallas kernels for 0%

commit v1 on v0

--- a/solution.py
+++ b/solution.py
@@ -85,7 +85,11 @@
     squares = jnp.sum(
         (difference * difference).reshape(src_blocks, batch, channels, width), axis=(0, 1, 3)
     )
-    sums = lax.psum(squares, "src")
+    n_dev = lax.axis_size("src")
+    sums, far = (squares, 1)
+    while far < n_dev:
+        sums = sums + lax.ppermute(sums, "src", [(i, i ^ far) for i in range(n_dev)])
+        far = 2 * far
     channel_rms = jnp.sqrt(sums / total_points + EPSILON)
     return (returned.reshape(source_field.shape), channel_rms)
 

time: 278 us -> 250 us (0.90)
  blocking collectives: 42 us -> 0 us
  starting transfers between devices: 0.08 us -> 8.16 us
  waiting for transfers between devices: 178 us -> 184 us
    psum x1 -> x0, blocking collectives: 42 us -> none  [body(): sums = lax.psum(squares, 'src')]
    ppermute x0 -> x4, starting transfers between devices: none -> 8.08 us  [body(): lax.ppermute(sums, 'src', [(i, i ^ far) for i in range(n_dev)])]
    ppermute x0 -> x4, waiting for transfers between devices: none -> 5.85 us  [body(): lax.ppermute(sums, 'src', [(i, i ^ far) for i in range(n_dev)])]
  transfers between devices with their start and end apart: 2 -> 6, of which waited for: 2 -> 6; matrix products, arithmetic and copies ran while one was open for 0% -> 1% of each run, Pallas kernels for 0% -> 0%
where the time goes in v1:
time: 250 us; the launch traced here: 249 us
  waiting for transfers between devices  184 us (74%)
  matrix products  22.2 us (9%)
  between operations  15.5 us (6%)
  other arithmetic  11.8 us (5%)
  starting transfers between devices  8.16 us (3%)
  local copies, waits for them, and re-layouts  7.72 us (3%)
    psum x1, waiting for transfers between devices, body(): lax.psum(partial_value, 'src')  159 us
    psum x1, waiting for transfers between devices, body(): returned = lax.psum(partial_back, 'hid')  18.3 us
    ppermute x4, starting transfers between devices, body(): lax.ppermute(sums, 'src', [(i, i ^ far) for i in range(n_dev)])  8.08 us
    dot_general x2, matrix products, decode_group(): product = jnp.einsum('tfr,trc->tfc', blocks, tiles, precision=HIGH)  6.31 us
    ppermute x4, waiting for transfers between devices, body(): lax.ppermute(sums, 'src', [(i, i ^ far) for i in range(n_dev)])  5.85 us
    dot_general x2, matrix products, decode_group(): jnp.einsum('ts,tfc->sfc', placing, product, precision=HIGH)  5.57 us
    unnamed x12, local copies, waits for them, and re-layouts  5.06 us
  transfers between devices with their start and end apart: 6, of which 6 were waited for; matrix products, arithmetic and copies ran while one was open for 1% of the time, Pallas kernels for 0%

profile of v1, /device:TPU:0, one launch (start us, length us, event | category | flops | bytes accessed | tf_op | source)
XLA Modules:
  0.0 249.1 jit_solution(4215097659516070779)
XLA Ops:
  7.2 0.0 all-reduce.3.cloned.1.call-start
  7.9 2.1 copy.23
  10.0 0.7 broadcast_subtract_fusion
  10.7 0.4 broadcast_in_dim.5
  11.1 8.7 %while.22 = (s32[]{:T(128)}, f32[32,196,128]{2,0,1:T(8,128)S(1)}, s32[]{:T(128)}, s32[1]{0:T(128)}, s32[32]{0:T(128)S(1)}, /*index=5*/s32[32]{0:T(128)S(1)}, f32...) while((s32[]{:T(128)}, f32[32,196,128]{2,0,1:T(8,128)S(1)}, ...), condition=%wide.region_1.2_spmd.clone, body=%wide.region_0.1_spmd.clone.sunk | while | flops 810042496 | bytes 23085684 | solution.py:58
  11.1 0.0 copy-start.1
  11.1 0.1 dynamic_slice.35
  11.2 2.1 fusion.73
  13.3 0.0 copy-done.1
  13.3 3.2 %fusion.74 = f32[16,196,128]{2,1,0:T(8,128)S(1)} fusion(f32[16,196,128]{2,0,1:T(8,128)S(1)} %fusion.73, f32[32,128,128]{2,1,0:T(8,128)S(1)} %copy-done.1, s32[]{:T(128)S(6)} %select_n.24), kind=kOutput, calls=%fused_computation.7.clone.1 | convolution fusion | flops 616562688 | bytes 4259844 | tf_op jit(solution)/shard_map/while/body/tfr,trc->tfc/dot_general | solution.py:54
  16.5 0.1 dynamic_slice.36
  16.5 0.7 fusion.75
  17.2 2.6 %convolution_add_fusion.2 = f32[32,196,128]{2,0,1:T(8,128)S(1)} fusion(f32[32,196,128]{2,0,1:T(8,128)S(1)} %get-tuple-element.339, f32[16,196,128]{2,1,0:T(8,128)S(1)} %fusion.74, s32[16]{0:T(128)S(1)} %dynamic_slice.36, pred[16]{0:T(512)(128)(4,1)S(1)} %fusion.75), kind=kOutput, calls=%fused_computation.6.clone.1 | convolution fusion | flops 154944512 | bytes 8028240 | tf_op jit(solution)/shard_map/while/body/th,tfc->hfc/dot_general | solution.py:55
  19.8 0.0 copy-start
  19.8 0.0 copy-start.6
  19.8 0.0 copy-start.4
  19.8 0.0 copy-start.5
  19.8 1.6 copy-done
  21.5 0.0 all-reduce.3.cloned.1.call-update
  21.5 0.0 all-reduce.5.cloned.1.call-start
  22.2 0.0 copy-done.6
  22.2 0.1 mul.48
  22.3 0.0 copy-done.4
  22.3 0.0 copy-done.5
  22.3 159.5 %all-reduce.3.cloned.1.call-done = f32[32,196,128]{2,0,1:T(8,128)} async-done(((f32[32,196,128]{2,0,1:T(8,128)}), f32[32,196,128]{2,0,1:T(8,128)}) %all-reduce.3.cloned.1.call-update) | async-done | bytes 3211280 | tf_op jit(solution)/shard_map/psum | solution.py:61
  181.8 3.6 %mul.51 = f32[32,196,128]{2,0,1:T(8,128)S(1)} multiply(f32[32,196,128]{2,0,1:T(8,128)} %all-reduce.3.cloned.1.call-done, f32[32,196,128]{2,0,1:T(8,128)} %all-reduce.3.cloned.1.call-done) | non-fusion elementwise | flops 802816 | bytes 9633792 | tf_op jit(solution)/shard_map/mul | solution.py:15
  185.4 0.2 reduce_sum.21
  185.7 2.2 bitcast_multiply_fusion
  187.9 0.9 broadcast_in_dim.4
  188.9 16.7 %while.23 = (s32[]{:T(128)}, f32[8,196,128]{2,0,1:T(8,128)}, s32[]{:T(128)}, s32[1]{0:T(128)}, s32[32]{0:T(128)S(1)}, /*index=5*/s32[32]{0:T(128)S(1)}, f32[32,1...) while((s32[]{:T(128)}, f32[8,196,128]{2,0,1:T(8,128)}, ...), condition=%wide.region_5.6_spmd.clone, body=%wide.region_4.5_spmd.clone.sunk | while | flops 809440000 | bytes 20677236 | solution.py:79
  188.9 0.1 dynamic_slice.38
  188.9 0.0 copy-start.2
  188.9 1.2 fusion.82
  190.2 0.3 copy-done.2
  190.5 3.2 %fusion.83 = f32[16,196,128]{2,1,0:T(8,128)S(1)} fusion(f32[16,196,128]{2,0,1:T(8,128)S(1)} %fusion.82, f32[32,128,128]{2,1,0:T(8,128)S(1)} %copy-done.2, s32[]{:T(128)S(6)} %select_n.25), kind=kOutput, calls=%fused_computation.23.clone.1 | convolution fusion | flops 616562688 | bytes 4259844 | tf_op jit(solution)/shard_map/while/body/tfr,trc->tfc/dot_general | solution.py:74
  193.7 0.1 dynamic_slice.39
  193.8 0.7 fusion.84
  194.4 2.8 %fusion.85 = f32[8,196,128]{2,0,1:T(8,128)} fusion(f32[8,196,128]{2,0,1:T(8,128)} %get-tuple-element.375, f32[16,196,128]{2,1,0:T(8,128)S(1)} %fusion.83, s32[16]{0:T(128)S(1)} %dynamic_slice.39, pred[16]{0:T(512)(128)(4,1)S(1)} %fusion.84), kind=kOutput, calls=%fused_computation.27.clone.1 | convolution fusion | flops 38736128 | bytes 3211344 | tf_op jit(solution)/shard_map/while/body/ts,tfc->sfc/dot_general | solution.py:76
  197.2 0.1 dynamic_slice.38
  197.3 0.0 copy-start.2
  197.3 1.2 fusion.82
  198.5 0.3 copy-done.2
  198.9 3.2 %fusion.83 = f32[16,196,128]{2,1,0:T(8,128)S(1)} fusion(f32[16,196,128]{2,0,1:T(8,128)S(1)} %fusion.82, f32[32,128,128]{2,1,0:T(8,128)S(1)} %copy-done.2, s32[]{:T(128)S(6)} %select_n.25), kind=kOutput, calls=%fused_computation.23.clone.1 | convolution fusion | flops 616562688 | bytes 4259844 | tf_op jit(solution)/shard_map/while/body/tfr,trc->tfc/dot_general | solution.py:74
  202.0 0.1 dynamic_slice.39
  202.1 0.7 fusion.84
  202.8 2.8 %fusion.85 = f32[8,196,128]{2,0,1:T(8,128)} fusion(f32[8,196,128]{2,0,1:T(8,128)} %get-tuple-element.375, f32[16,196,128]{2,1,0:T(8,128)S(1)} %fusion.83, s32[16]{0:T(128)S(1)} %dynamic_slice.39, pred[16]{0:T(512)(128)(4,1)S(1)} %fusion.84), kind=kOutput, calls=%fused_computation.27.clone.1 | convolution fusion | flops 38736128 | bytes 3211344 | tf_op jit(solution)/shard_map/while/body/ts,tfc->sfc/dot_general | solution.py:76
  205.6 0.0 all-reduce.5.cloned.1.call-update
  205.6 18.3 %all-reduce.5.cloned.1.call-done = f32[8,196,128]{2,0,1:T(8,128)} async-done(((f32[8,196,128]{2,0,1:T(8,128)}), f32[8,196,128]{2,0,1:T(8,128)}) %all-reduce.5.cloned.1.call-update) | async-done | bytes 802832 | tf_op jit(solution)/shard_map/psum | solution.py:83
  223.9 0.0 copy-start.3
  223.9 2.5 multiply_reduce_fusion
  226.4 0.1 reduce_sum.27
  226.5 1.8 collective-permute-start
  228.3 1.8 collective-permute-done
  230.1 1.8 collective-permute-start.1
  231.9 1.8 collective-permute-done.1
  233.7 1.8 collective-permute-start.2
  235.4 1.8 collective-permute-done.2
  237.2 2.7 %collective-permute-start.3 = (f32[98]{0:T(128)S(1)}, f32[98]{0:T(128)S(1)}, u32[]{:S(2)}, u32[]{:S(2)}) collective-permute-start(f32[98]{0:T(128)S(1)} %add.91), channel_id=1, source_target_pairs={{0,16},{2,18},{4,20},{6,22},{8,24},{10,26},{12,28},{14,30},{16,0},... | collective-permute-start | bytes 1184 | tf_op jit(solution)/shard_map/ppermute | solution.py:91
  239.9 0.0 copy-done.3
  239.9 1.3 copy.24
  241.2 0.5 collective-permute-done.3
  241.7 0.5 add_sqrt_fusion
  (7 shorter events, 0.1 us)
Async XLA Ops:
  7.2 174.6 %all-reduce.3.cloned.1.call-start = ((), (), s32[]{:S(2)}) async-start(), calls=%async_computation | async-start | bytes 6422528 | tf_op jit(solution)/shard_map/psum | solution.py:61
  11.1 2.2 copy-start.1
  19.8 1.7 copy-start
  19.8 2.4 copy-start.6
  19.8 2.5 %copy-start.4 = (s32[32]{0:T(128)S(1)}, s32[32]{0:T(128)}, u32[]{:S(2)}) copy-start(s32[32]{0:T(128)} %param.22) | copy-start | bytes 388
  19.8 2.5 copy-start.5
  21.5 202.4 %all-reduce.5.cloned.1.call-start = ((), (), s32[]{:S(2)}) async-start(), calls=%async_computation.1 | async-start | bytes 1605632 | tf_op jit(solution)/shard_map/psum | solution.py:83
  188.9 1.6 copy-start.2
  197.3 1.6 copy-start.2
  223.9 16.1 %copy-start.3 = (f32[8,196,128]{2,0,1:T(8,128)S(1)}, f32[8,196,128]{2,0,1:T(8,128)}, u32[]{:S(2)}) copy-start(f32[8,196,128]{2,0,1:T(8,128)} %all-reduce.5.cloned.1.call-done) | copy-start | bytes 2408452
  226.5 3.6 %collective-permute-start = (f32[98]{0:T(128)S(1)}, f32[98]{0:T(128)S(1)}, u32[]{:S(2)}, u32[]{:S(2)}) collective-permute-start(f32[98]{0:T(128)S(1)} %reduce_sum.28), channel_id=1, source_target_pairs={{0,2},{2,0},{4,6},{6,4},{8,10},{10,8},{12,14},{14,12},{16,18},{18,... | collective-permute-start | bytes 1184 | tf_op jit(solution)/shard_map/ppermute | solution.py:91
  230.1 3.6 %collective-permute-start.1 = (f32[98]{0:T(128)S(1)}, f32[98]{0:T(128)S(1)}, u32[]{:S(2)}, u32[]{:S(2)}) collective-permute-start(f32[98]{0:T(128)S(1)} %add.89), channel_id=1, source_target_pairs={{0,4},{2,6},{4,0},{6,2},{8,12},{10,14},{12,8},{14,10},{16,20},{18,... | collective-permute-start | bytes 1184 | tf_op jit(solution)/shard_map/ppermute | solution.py:91
  233.7 3.6 %collective-permute-start.2 = (f32[98]{0:T(128)S(1)}, f32[98]{0:T(128)S(1)}, u32[]{:S(2)}, u32[]{:S(2)}) collective-permute-start(f32[98]{0:T(128)S(1)} %add.90), channel_id=1, source_target_pairs={{0,8},{2,10},{4,12},{6,14},{8,0},{10,2},{12,4},{14,6},{16,24},{18,... | collective-permute-start | bytes 1184 | tf_op jit(solution)/shard_map/ppermute | solution.py:91
  237.2 4.5 %collective-permute-start.3 = (f32[98]{0:T(128)S(1)}, f32[98]{0:T(128)S(1)}, u32[]{:S(2)}, u32[]{:S(2)}) collective-permute-start(f32[98]{0:T(128)S(1)} %add.91), channel_id=1, source_target_pairs={{0,16},{2,18},{4,20},{6,22},{8,24},{10,26},{12,28},{14,30},{16,0},... | collective-permute-start | bytes 1184 | tf_op jit(solution)/shard_map/ppermute | solution.py:91
Sparse Core Ops, SparseCore 0:
  21.6 160.1 all-reduce.2
  205.7 18.1 all-reduce.4
